TPU v7x, 32 devices: a whole 2x2x4 slice. The times are simulated.
32 devices in a mesh: row: 2 (over core), sa: 16 (over z, y, x).
Axes of the slice: x: 2, y: 2, z: 4, core: 2. Of those that a mesh axis runs over, the one named last changes fastest.
Arguments:
- rep_w1: float32 [4, 2, 64, 4096], P('row', None, None, 'sa'), may hold values from -6 to 6
- rep_w3: float32 [4, 2, 64, 4096], P('row', None, None, 'sa'), may hold values from -6 to 6
- rep_w2: float32 [4, 2, 64, 4096], P('row', None, None, 'sa'), may hold values from -6 to 6
- rep_gate: float32 [4, 2, 4096], P('row', None, 'sa'), may hold values from -6 to 6
Outputs:
- serve_w1: bfloat16 [2, 64, 4096], P('row', 'sa')
- serve_w3: bfloat16 [2, 64, 4096], P('row', 'sa')
- serve_w2: bfloat16 [2, 64, 4096], P('row', 'sa')
- serve_gate: bfloat16 [2, 4096], replicated
- soup_norms: float32 [2, 4], P('row')
- replica_norms: float32 [4, 2, 4], P('row')
All inputs are finite; a program needn't handle non-finite values.
Results may differ from a plain program's by a relative error of at most 0.001.
Values may be sent and summed in bfloat16 or wider, within the bound.
A program may use at most 64 MiB of HBM per device.

v0:
```python
import jax
import jax.numpy as jnp
from jax import lax
from jax.sharding import PartitionSpec as P


def own_rows_2(product, width, axis):
    everything = product(jnp.int32(0), lax.axis_size(axis) * width)
    own = lax.psum_scatter(everything, axis, scatter_dimension=0, tiled=True)
    return own


def square_sums(values, dims_summed):
    return jnp.sum(values * values, axis=dims_summed)


def local(rep_w1, rep_w3, rep_w2, rep_gate):
    rows_total = lax.axis_size("row")
    replicas = rep_w1.shape[0] * rows_total
    experts_all = rep_w1.shape[1]
    expert_rows = experts_all // rows_total
    hidden_all = rep_w1.shape[2]
    model_width = rep_w1.shape[3] * lax.axis_size("sa")
    weights = (rep_w1, rep_w3, rep_w2)
    replica_parts = jnp.stack(
        [square_sums(weight, (2, 3)) for weight in weights] + [square_sums(rep_gate, 2)], axis=2
    )

    def expert_terms(offset, length):
        pieces = [
            jnp.sum(lax.dynamic_slice_in_dim(weight, offset, length, 1), axis=0)
            for weight in weights
        ]
        return jnp.stack(pieces, axis=1)

    summed = own_rows_2(expert_terms, expert_rows, "row")
    served = (summed / replicas).astype(jnp.bfloat16)
    arranged = lax.all_to_all(served, "sa", split_axis=2, concat_axis=3, tiled=True)
    served_list = [arranged[:, column] for column in range(3)]
    gate_local = jnp.sum(rep_gate, axis=0)
    gate_total = lax.psum(gate_local, "row")
    gate_shard = (gate_total / replicas).astype(jnp.bfloat16)
    serve_gate = lax.all_gather(gate_shard, "sa", axis=1, tiled=True)
    own_rows = lax.dynamic_slice_in_dim(
        gate_shard, lax.axis_index("row") * expert_rows, expert_rows, 0
    )
    soup_parts = jnp.stack(
        [square_sums(served.astype(jnp.float32), (1, 2)) for served in served_list]
        + [square_sums(own_rows.astype(jnp.float32), 1)],
        axis=1,
    )
    replica_total, soup_total = lax.psum((replica_parts, soup_parts), "sa")
    counts = jnp.array([hidden_all * model_width] * 3 + [model_width], jnp.float32)
    replica_norms = jnp.sqrt(replica_total / counts)
    soup_norms = jnp.sqrt(soup_total / counts)
    return (served_list[0], served_list[1], served_list[2], serve_gate, soup_norms, replica_norms)


def solution(mesh):
    placed = (
        P("row", None, None, "sa"),
        P("row", None, None, "sa"),
        P("row", None, None, "sa"),
        P("row", None, "sa"),
    )
    return jax.shard_map(
        local,
        mesh=mesh,
        in_specs=placed,
        out_specs=(
            P("row", "sa", None),
            P("row", "sa", None),
            P("row", "sa", None),
            P(),
            P("row", None),
            P("row", None, None),
        ),
        check_vma=False,
    )
```

profile of v0, /device:TPU:0, one launch (start us, length us, event | category | flops | bytes accessed | tf_op | source)
XLA Modules:
  0.0 122.1 jit_solution(15603964799628544858)
XLA Ops:
  7.2 0.0 copy-start
  7.2 0.0 reduce-scatter.2.cloned.1.call-start
  7.2 1.1 multiply_reduce_fusion.2
  8.3 0.0 copy-done
  8.3 1.1 multiply_reduce_fusion
  9.5 0.8 copy.15
  10.3 0.0 copy-start.1
  10.3 0.0 reduce-scatter.2.cloned.1.call-update
  10.3 0.7 copy-done.1
  11.0 0.1 multiply_reduce_fusion.6
  11.0 2.6 %psum.21 = f32[2,256]{1,0:T(2,128)S(1)} all-reduce(f32[2,256]{1,0:T(2,128)S(1)} %get-tuple-element.37), channel_id=1, replica_groups=mesh['row'=2,'sa'=16] {'row'}, use_global_device_ids=true, to_apply=%region_5.0 | all-reduce | flops 512 | bytes 4096 | tf_op jit(solution)/shard_map/psum | solution.py:41
  13.7 7.4 %reduce-scatter.2.cloned.1.call-done = f32[1,3,64,256]{3,2,1,0:T(8,128)} async-done(((f32[2,3,64,256]{3,2,1,0:T(8,128)}), f32[1,3,64,256]{3,2,1,0:T(8,128)}) %reduce-scatter.2.cloned.1.call-update) | async-done | bytes 196624 | tf_op jit(solution)/shard_map/reduce_scatter | solution.py:9
  21.0 0.9 multiply_convert_fusion
  22.0 0.7 copy.16
  22.7 6.7 %all-to-all-start = ((bf16[1,3,64,256]{3,1,0,2:T(4,128)(2,1)}), bf16[1,3,64,256]{3,1,0,2:T(4,128)(2,1)S(1)}, u32[]{:S(2)}, u32[]{:S(2)}) async-start(bf16[1,3,64,256]{3,1,0,2:T(4,128)(2,1)} %copy.16), calls=%async_computation.1 | async-start | bytes 262144 | tf_op jit(solution)/shard_map/all_to_all | solution.py:38
  29.4 0.6 multiply_reduce_fusion.7
  30.0 41.1 %all_gather.3 = bf16[2,4096]{1,0:T(2,128)(2,1)S(1)} all-gather(bf16[2,256]{1,0:T(2,128)(2,1)S(1)} %multiply_convert_fusion.1), channel_id=1, replica_groups=mesh['row'=2,'sa'=16] {'sa'}, dimensions={1}, use_global_device_ids=true | all-gather | bytes 17408 | tf_op jit(solution)/shard_map/all_gather | solution.py:43
  71.1 0.0 all-to-all-done
  71.2 1.3 %multiply_reduce_fusion.3 = (f32[]{:T(128)}, bf16[1,4,4096]{2,1,0:T(4,128)(2,1)}, f32[]{:T(128)}, bf16[1,4,4096]{2,1,0:T(4,128)(2,1)}, f32[]{:T(128)}, /*index=5*/bf16[1,4,4096]{2,1,0:T(4,128)(2,1)}) fusion(bf16[1,3,4,4096]{3,2,1,0:T(4,128)(2,1)S(1)} %bitcast.28), kind=kLoop, calls=%fused_computation.5 | loop fusion | flops 147453 | bytes 196620 | tf_op jit(solution)/shard_map/reduce_sum | solution.py:14
  72.5 2.6 %pad_maximum_fusion.2 = f32[1,4]{1,0:T(1,128)S(1)} fusion(f32[1,1]{1,0:T(1,128)} %bitcast.13, f32[1,1]{1,0:T(1,128)} %bitcast.12, f32[1,1]{1,0:T(1,128)} %bitcast.11, f32[1,1]{1,0:T(1,128)} %bitcast.10), kind=kLoop, calls=%fused_computation.16 | loop fusion | flops 12 | bytes 32 | tf_op jit(solution)/shard_map/stack | solution.py:47
  75.0 37.0 %all-reduce = (f32[1,4]{1,0:T(1,128)S(1)}, f32[2,2,4]{1,0,2:T(2,128)S(1)}) all-reduce(f32[1,4]{1,0:T(1,128)S(1)} %pad_maximum_fusion.2, f32[2,2,4]{1,0,2:T(2,128)S(1)} %pad_maximum_fusion.1), channel_id=1, replica_groups=mesh['row'=2,'sa'=16] {'sa'}, use_global_device_ids=true, to_apply=%region_10.0 | all-reduce | flops 20 | bytes 160 | tf_op jit(solution)/shard_map/psum | solution.py:52
  112.1 0.0 copy-start.2
  112.1 0.6 copy-done.2
  112.7 0.1 multiply_sqrt_fusion
  112.8 0.7 copy.18
  113.5 0.0 copy-start.3
  113.5 0.7 copy-done.3
  114.2 0.5 multiply_sqrt_fusion.1
  114.7 0.6 copy.21
  (4 shorter events, 0.1 us)
Async XLA Ops:
  7.2 1.2 copy-start
  7.2 13.9 %reduce-scatter.2.cloned.1.call-start = ((), (), s32[]{:S(2)}) async-start(), calls=%async_computation.2 | async-start | bytes 589824 | tf_op jit(solution)/shard_map/reduce_scatter | solution.py:9
  10.3 0.7 copy-start.1
  22.7 48.4 %all-to-all-start = ((bf16[1,3,64,256]{3,1,0,2:T(4,128)(2,1)}), bf16[1,3,64,256]{3,1,0,2:T(4,128)(2,1)S(1)}, u32[]{:S(2)}, u32[]{:S(2)}) async-start(bf16[1,3,64,256]{3,1,0,2:T(4,128)(2,1)} %copy.16), calls=%async_computation.1 | async-start | bytes 262144 | tf_op jit(solution)/shard_map/all_to_all | solution.py:38
  112.1 0.7 copy-start.2
  113.5 0.7 copy-start.3
Sparse Core Ops, SparseCore 0:
  10.4 10.5 reduce-scatter.1
where the time goes:
time: 123 us; the launch traced here: 122 us
  blocking collectives  80.7 us (66%)
  between operations  14.1 us (11%)
  other arithmetic  8.38 us (7%)
  waiting for transfers between devices  7.38 us (6%)
  starting transfers between devices  6.76 us (5%)
  local copies, waits for them, and re-layouts  4.79 us (4%)
    all_gather x1, blocking collectives, local(): serve_gate = lax.all_gather(gate_shard, 'sa', axis=1, tiled=True)  41.1 us
    psum x1, blocking collectives, local(): replica_total, soup_total = lax.psum((replica_parts, soup_parts), 'sa')  37 us
    reduce_scatter x1, waiting for transfers between devices, own_rows_2(): own = lax.psum_scatter(everything, axis, scatter_dimension=0, tiled=True)  7.36 us
    all_to_all x1, starting transfers between devices, local(): lax.all_to_all(served, 'sa', split_axis=2, concat_axis=3, tiled=True)  6.72 us
    reduce_sum x5, other arithmetic, square_sums(): return jnp.sum(values * values, axis=dims_summed)  4.24 us
    unnamed x10, local copies, waits for them, and re-layouts  3.25 us
    psum x1, blocking collectives, local(): gate_total = lax.psum(gate_local, 'row')  2.62 us
    another operation x1, other arithmetic, local(): jnp.stack([square_sums(served.astype(jnp.float32), (1, 2)) for served in...  2.57 us
  transfers between devices with their start and end apart: 2, of which 1 were waited for; matrix products, arithmetic and copies ran while one was open for 1% of the time, Pallas kernels for 0%

commit v1 on v0

v1 whole, which is shorter than its diff:
```python
import functools

import jax
import jax.numpy as jnp
from jax import lax
from jax.experimental import pallas as pl
from jax.experimental.pallas import tpu as pltpu
from jax.sharding import PartitionSpec as P

MESH = pl.DeviceIdType.MESH
F32 = jnp.float32
BF16 = jnp.bfloat16


def scaled(total, replicas):
    if replicas & (replicas - 1) == 0:
        return total * (1.0 / replicas)
    return total / replicas


def square_sum(values):
    squares = values * values
    while squares.ndim > 2:
        squares = jnp.sum(squares, axis=0)
    rows = jnp.sum(squares, axis=0, keepdims=True)
    return jnp.sum(rows, axis=1, keepdims=True)


def kernel(
    rows, n, replicas, counts,
    w1_hbm, w3_hbm, w2_hbm, gate_hbm,
    out1, out3, out2, gate_out, soup_out, rep_out,
    w_in, gate_in, part, part_got, gate_slots, block, gate_block, stats_send, stats_slots,
    in_sem, row_send, row_recv, gate_row_send, gate_row_recv, sa_send, sa_recv,
):
    sources = (w1_hbm, w3_hbm, w2_hbm)
    outs = (out1, out3, out2)
    held, experts, hidden, width = w1_hbm.shape
    own_experts = experts // rows
    own_hidden = hidden // n
    row = lax.axis_index("row")
    me = lax.axis_index("sa")

    loads = [pltpu.make_async_copy(gate_hbm, gate_in, in_sem.at[3])]
    loads += [pltpu.make_async_copy(sources[t], w_in.at[t], in_sem.at[t]) for t in range(3)]
    for load in loads:
        load.start()

    barrier = pltpu.get_barrier_semaphore()

    def greet(step, carry):
        pl.semaphore_signal(
            barrier, inc=1, device_id={"sa": lax.rem(me + step, n)}, device_id_type=MESH
        )
        return carry

    for step in range(1, rows):
        pl.semaphore_signal(
            barrier, inc=1, device_id={"row": lax.rem(row + step, rows)}, device_id_type=MESH
        )
    lax.fori_loop(1, n, greet, 0)

    lane = lax.broadcasted_iota(jnp.int32, (1, stats_send.shape[1]), 1)
    stats = jnp.zeros((1, stats_send.shape[1]), F32)
    soup_lanes = 4 * own_experts

    def rep_lane(replica, expert, t):
        return soup_lanes + 4 * (replica * experts + expert) + t

    loads[0].wait()
    gate_sum = gate_in[0]
    for replica in range(1, held):
        gate_sum = gate_sum + gate_in[replica]
    gate_slots[row] = gate_sum
    for t in range(3):
        loads[1 + t].wait()
        for step in range(1, rows):
            first = lax.rem(row + step, rows) * own_experts
            total = w_in[t, 0, pl.ds(first, own_experts)]
            for replica in range(1, held):
                total = total + w_in[t, replica, pl.ds(first, own_experts)]
            part[t, step - 1] = total

    pl.semaphore_wait(barrier, rows - 1 + n - 1)

    gate_copies = []
    part_copies = []
    for step in range(1, rows):
        gate_copies.append(
            pltpu.make_async_remote_copy(
                src_ref=gate_slots.at[row],
                dst_ref=gate_slots.at[row],
                send_sem=gate_row_send.at[step - 1],
                recv_sem=gate_row_recv.at[step - 1],
                device_id={"row": lax.rem(row + step, rows)},
                device_id_type=MESH,
            )
        )
        gate_copies[-1].start()
    for t in range(3):
        for step in range(1, rows):
            part_copies.append(
                pltpu.make_async_remote_copy(
                    src_ref=part.at[t, step - 1],
                    dst_ref=part_got.at[t, step - 1],
                    send_sem=row_send.at[t, step - 1],
                    recv_sem=row_recv.at[t, step - 1],
                    device_id={"row": lax.rem(row + step, rows)},
                    device_id_type=MESH,
                )
            )
            part_copies[-1].start()

    for replica in range(held):
        for expert in range(experts):
            for t in range(3):
                stats = jnp.where(
                    lane == rep_lane(replica, expert, t),
                    square_sum(w_in[t, replica, expert]),
                    stats,
                )
            stats = jnp.where(
                lane == rep_lane(replica, expert, 3),
                square_sum(gate_in[replica, pl.ds(expert, 1)]),
                stats,
            )

    columns = pl.ds(pl.multiple_of(me * width, width), width)
    own_first = row * own_experts

    for copy in gate_copies:
        copy.wait_recv()
    gate_total = gate_slots[0]
    for other in range(1, rows):
        gate_total = gate_total + gate_slots[other]
    served_gate = scaled(gate_total, replicas).astype(BF16)
    gate_block[...] = served_gate
    gate_out[:, columns] = served_gate

    def send_gate(step, carry):
        pltpu.make_async_remote_copy(
            src_ref=gate_block,
            dst_ref=gate_out.at[:, columns],
            send_sem=sa_send.at[3],
            recv_sem=sa_recv.at[3],
            device_id={"sa": lax.rem(me + step, n)},
            device_id_type=MESH,
        ).start()
        return carry

    lax.fori_loop(1, n, send_gate, 0)

    gate_wide = served_gate.astype(F32)
    gate_squares = jnp.sum(gate_wide * gate_wide, axis=1, keepdims=True)
    expert_row = lax.broadcasted_iota(jnp.int32, gate_squares.shape, 0)
    for own in range(own_experts):
        square = jnp.sum(
            jnp.where(expert_row == own_first + own, gate_squares, 0.0), axis=0, keepdims=True
        )
        stats = jnp.where(lane == 4 * own + 3, square, stats)

    for t in range(3):
        for copy in part_copies[t * (rows - 1):(t + 1) * (rows - 1)]:
            copy.wait_recv()
        total = w_in[t, 0, pl.ds(own_first, own_experts)]
        for replica in range(1, held):
            total = total + w_in[t, replica, pl.ds(own_first, own_experts)]
        for step in range(1, rows):
            total = total + part_got[t, step - 1]
        served = scaled(total, replicas).astype(BF16)
        for dest in range(n):
            block[t, dest] = served[:, dest * own_hidden:(dest + 1) * own_hidden]

        def send_block(step, carry, t=t):
            peer = lax.rem(me + step, n)
            pltpu.make_async_remote_copy(
                src_ref=block.at[t, peer],
                dst_ref=outs[t].at[:, :, columns],
                send_sem=sa_send.at[t],
                recv_sem=sa_recv.at[t],
                device_id={"sa": peer},
                device_id_type=MESH,
            ).start()
            return carry

        lax.fori_loop(1, n, send_block, 0)
        outs[t][:, :, columns] = block[t, me]
        for own in range(own_experts):
            stats = jnp.where(
                lane == 4 * own + t, square_sum(served[own].astype(F32)), stats
            )

    stats_send[...] = stats
    stats_slots[me] = stats

    def send_stats(step, carry):
        pltpu.make_async_remote_copy(
            src_ref=stats_send,
            dst_ref=stats_slots.at[me],
            send_sem=sa_send.at[4],
            recv_sem=sa_recv.at[4],
            device_id={"sa": lax.rem(me + step, n)},
            device_id_type=MESH,
        ).start()
        return carry

    lax.fori_loop(1, n, send_stats, 0)

    others = pl.ds(0, (n - 1) * width)
    landed = [outs[t].at[:, :, others] for t in range(3)]
    landed += [gate_out.at[:, others], stats_slots.at[pl.ds(0, n - 1)]]
    pltpu.make_async_copy(landed[4], landed[4], sa_recv.at[4]).wait()
    norms = stats_slots[0]
    for source in range(1, n):
        norms = norms + stats_slots[source]
    norms = jnp.sqrt(jnp.where(lane % 4 == 3, norms / counts[1], norms / counts[0]))
    for own in range(own_experts):
        soup_out[pl.ds(own, 1), :] = norms[:, 4 * own:4 * own + 4]
    for replica in range(held):
        for expert in range(experts):
            at = rep_lane(replica, expert, 0)
            rep_out[replica, pl.ds(expert, 1), :] = norms[:, at:at + 4]

    for t in (3, 0, 1, 2):
        pltpu.make_async_copy(landed[t], landed[t], sa_recv.at[t]).wait()
    for copy in gate_copies + part_copies:
        copy.wait_send()
    for t in range(5):
        pltpu.make_async_copy(landed[t], landed[t], sa_send.at[t]).wait()


def local(rep_w1, rep_w3, rep_w2, rep_gate, rows, n):
    held, experts, hidden, width = rep_w1.shape
    own_experts, own_hidden = experts // rows, hidden // n
    lanes = -(-4 * (own_experts + held * experts) // 128) * 128
    vmem = pl.BlockSpec(memory_space=pltpu.VMEM)
    served = jax.ShapeDtypeStruct((own_experts, own_hidden, n * width), BF16)
    return pl.pallas_call(
        functools.partial(
            kernel, rows, n, held * rows, (float(hidden * width * n), float(width * n))
        ),
        out_shape=(
            served,
            served,
            served,
            jax.ShapeDtypeStruct((experts, n * width), BF16),
            jax.ShapeDtypeStruct((own_experts, 4), F32),
            jax.ShapeDtypeStruct((held, experts, 4), F32),
        ),
        in_specs=[pl.BlockSpec(memory_space=pl.ANY)] * 4,
        out_specs=(vmem,) * 6,
        scratch_shapes=[
            pltpu.VMEM((3, held, experts, hidden, width), F32),
            pltpu.VMEM((held, experts, width), F32),
            pltpu.VMEM((3, rows - 1, own_experts, hidden, width), F32),
            pltpu.VMEM((3, rows - 1, own_experts, hidden, width), F32),
            pltpu.VMEM((rows, experts, width), F32),
            pltpu.VMEM((3, n, own_experts, own_hidden, width), BF16),
            pltpu.VMEM((experts, width), BF16),
            pltpu.VMEM((1, lanes), F32),
            pltpu.VMEM((n, 1, lanes), F32),
            pltpu.SemaphoreType.DMA((4,)),
            pltpu.SemaphoreType.DMA((3, rows - 1)),
            pltpu.SemaphoreType.DMA((3, rows - 1)),
            pltpu.SemaphoreType.DMA((rows - 1,)),
            pltpu.SemaphoreType.DMA((rows - 1,)),
            pltpu.SemaphoreType.DMA((5,)),
            pltpu.SemaphoreType.DMA((5,)),
        ],
        compiler_params=pltpu.CompilerParams(collective_id=0, has_side_effects=True),
    )(rep_w1, rep_w3, rep_w2, rep_gate)


def solution(mesh):
    weights = P("row", None, None, "sa")
    return jax.shard_map(
        functools.partial(local, rows=mesh.shape["row"], n=mesh.shape["sa"]),
        mesh=mesh,
        in_specs=(weights, weights, weights, P("row", None, "sa")),
        out_specs=(
            P("row", "sa", None),
            P("row", "sa", None),
            P("row", "sa", None),
            P(),
            P("row", None),
            P("row", None, None),
        ),
        check_vma=False,
    )
```

time: 123 us -> 18.9 us (0.15)
  blocking collectives: 80.7 us -> 0 us
  between operations: 14.1 us -> 0.66 us
  Pallas kernels: 0 us -> 13.3 us
  other arithmetic: 8.38 us -> 0 us
  waiting for transfers between devices: 7.38 us -> 0 us
  starting transfers between devices: 6.76 us -> 0 us
    all_gather x1 -> x0, blocking collectives: 41.1 us -> none  [local(): serve_gate = lax.all_gather(gate_shard, 'sa', axis=1, tiled=True)]
    psum x2 -> x0, blocking collectives: 39.7 us -> none  [the longest x1 37 us: local(): replica_total, soup_total = lax.psum((replica_parts, soup_parts), 'sa')]
    pallas_call x0 -> x1, Pallas kernels: none -> 13.3 us  [local(): pl.pallas_call(functools.partial(kernel, rows, n, held * rows, (float(hid...]
    reduce_scatter x1 -> x0, waiting for transfers between devices: 7.36 us -> none  [own_rows_2(): own = lax.psum_scatter(everything, axis, scatter_dimension=0, tiled=True)]
    all_to_all x1 -> x0, starting transfers between devices: 6.72 us -> none  [local(): lax.all_to_all(served, 'sa', split_axis=2, concat_axis=3, tiled=True)]
    reduce_sum x5 -> x0, other arithmetic: 4.24 us -> none  [square_sums(): return jnp.sum(values * values, axis=dims_summed)]
    another operation x3 -> x0, other arithmetic: 2.6 us -> none  [the longest x1 2.57 us: local(): jnp.stack([square_sums(served.astype(jnp.float32), (1, 2)) for served in...]
    unnamed x10 -> x16, local copies, waits for them, and re-layouts: 3.25 us -> 4.59 us
  transfers between devices with their start and end apart: 2 -> 0, of which waited for: 1 -> 0; matrix products, arithmetic and copies ran while one was open for 1% -> 0% of each run, Pallas kernels for 0% -> 0%
where the time goes in v1:
time: 18.9 us; the launch traced here: 18.6 us
  Pallas kernels  13.3 us (70%)
  local copies, waits for them, and re-layouts  4.59 us (24%)
  between operations  0.66 us (3%)
    pallas_call x1, Pallas kernels, local(): pl.pallas_call(functools.partial(kernel, rows, n, held * rows, (float(hid...  13.3 us
    unnamed x16, local copies, waits for them, and re-layouts  4.59 us

profile of v1, /device:TPU:0, one launch (start us, length us, event | category | flops | bytes accessed | tf_op | source)
XLA Modules:
  0.0 18.6 jit_solution(6637314113951211297)
XLA Ops:
  0.6 13.3 %shard_map.91 = (bf16[1,4,4096]{2,1,0:T(4,128)(2,1)}, bf16[1,4,4096]{2,1,0:T(4,128)(2,1)}, bf16[1,4,4096]{2,1,0:T(4,128)(2,1)}, bf16[2,4096]{1,0:T(2,128)(2,1)}, f32[1,4]{1,0:T(1,128)}, /*index=5*/f32[2,2,4]{2,1,0:T(2,128)}) custom-call(f32[2,2,64,256]{3,2,1,0:T(8,128)} %w1_hbm.1, f32[2,2,64,256]{3,2,1,0:T(8,128)} %w3_hbm.1, f32[2,2,64,256]{3,2,1,0:T(8,128)} %w2_hbm.1, ...), custom_call_target="tpu_custom_call" | custom-call | tf_op jit(solution)/shard_map/pallas_call | solution.py:238
  13.9 0.0 copy-start.1
  14.0 1.4 %copy.16 = bf16[1,4,4096]{2,1,0:T(4,128)(2,1)} copy(bf16[1,4,4096]{2,1,0:T(4,128)(2,1)} %get-tuple-element.12) | data formatting | bytes 65536
  15.3 0.0 copy-done.1
  15.3 0.0 copy-start
  15.3 0.6 %copy.17 = bf16[1,4,4096]{2,1,0:T(4,128)(2,1)} copy(bf16[1,4,4096]{2,1,0:T(4,128)(2,1)S(1)} %copy-done.1) | data formatting | bytes 65536
  16.0 0.2 copy-done
  16.1 0.0 copy-start.2
  16.1 0.6 %copy.18 = bf16[1,4,4096]{2,1,0:T(4,128)(2,1)} copy(bf16[1,4,4096]{2,1,0:T(4,128)(2,1)S(1)} %copy-done) | data formatting | bytes 65536
  16.7 0.1 copy-done.2
  16.8 0.0 copy-start.4
  16.9 0.0 copy-start.3
  16.9 0.6 %copy.19 = bf16[2,4096]{1,0:T(2,128)(2,1)} copy(bf16[2,4096]{1,0:T(2,128)(2,1)S(1)} %copy-done.2) | data formatting | bytes 32768
  17.5 0.0 copy-done.4
  17.5 0.5 %copy.20 = f32[1,4]{1,0:T(1,128)} copy(f32[1,4]{1,0:T(1,128)S(1)} %copy-done.4) | data formatting | bytes 32
  18.0 0.0 copy-done.3
  18.0 0.6 %copy.21 = f32[2,2,4]{2,1,0:T(2,128)} copy(f32[2,2,4]{2,1,0:T(2,128)S(1)} %copy-done.3) | data formatting | bytes 128
Async XLA Ops:
  13.9 1.4 %copy-start.1 = (bf16[1,4,4096]{2,1,0:T(4,128)(2,1)S(1)}, bf16[1,4,4096]{2,1,0:T(4,128)(2,1)}, u32[]{:S(2)}) copy-start(bf16[1,4,4096]{2,1,0:T(4,128)(2,1)} %get-tuple-element.13) | copy-start | bytes 98308
  15.3 0.8 %copy-start = (bf16[1,4,4096]{2,1,0:T(4,128)(2,1)S(1)}, bf16[1,4,4096]{2,1,0:T(4,128)(2,1)}, u32[]{:S(2)}) copy-start(bf16[1,4,4096]{2,1,0:T(4,128)(2,1)} %get-tuple-element.14) | copy-start | bytes 98308
  16.1 0.7 %copy-start.2 = (bf16[2,4096]{1,0:T(2,128)(2,1)S(1)}, bf16[2,4096]{1,0:T(2,128)(2,1)}, u32[]{:S(2)}) copy-start(bf16[2,4096]{1,0:T(2,128)(2,1)} %get-tuple-element.15) | copy-start | bytes 49156
  16.8 0.6 %copy-start.4 = (f32[1,4]{1,0:T(1,128)S(1)}, f32[1,4]{1,0:T(1,128)}, u32[]{:S(2)}) copy-start(f32[1,4]{1,0:T(1,128)} %get-tuple-element.16) | copy-start | bytes 52
  16.9 1.1 %copy-start.3 = (f32[2,2,4]{2,1,0:T(2,128)S(1)}, f32[2,2,4]{2,1,0:T(2,128)}, u32[]{:S(2)}) copy-start(f32[2,2,4]{2,1,0:T(2,128)} %get-tuple-element.17) | copy-start | bytes 196

commit v2 on v1

--- a/solution.py
+++ b/solution.py
@@ -10,6 +10,7 @@
 MESH = pl.DeviceIdType.MESH
 F32 = jnp.float32
 BF16 = jnp.bfloat16
+VMEM_LIMIT = 40 * 1024 * 1024
 
 
 def scaled(total, replicas):
@@ -229,13 +230,35 @@
         pltpu.make_async_copy(landed[t], landed[t], sa_send.at[t]).wait()
 
 
+def finish_kernel(*refs):
+    count = (len(refs) - 1) // 2
+    copies = [
+        pltpu.make_async_copy(refs[i], refs[count + i], refs[-1].at[i]) for i in range(count)
+    ]
+    for copy in copies:
+        copy.start()
+    for copy in copies:
+        copy.wait()
+
+
+def finish(results):
+    return pl.pallas_call(
+        finish_kernel,
+        out_shape=tuple(jax.ShapeDtypeStruct(r.shape, r.dtype) for r in results),
+        in_specs=[pl.BlockSpec(memory_space=pltpu.VMEM)] * len(results),
+        out_specs=(pl.BlockSpec(memory_space=pltpu.HBM),) * len(results),
+        scratch_shapes=[pltpu.SemaphoreType.DMA((len(results),))],
+        compiler_params=pltpu.CompilerParams(vmem_limit_bytes=VMEM_LIMIT),
+    )(*results)
+
+
 def local(rep_w1, rep_w3, rep_w2, rep_gate, rows, n):
     held, experts, hidden, width = rep_w1.shape
     own_experts, own_hidden = experts // rows, hidden // n
     lanes = -(-4 * (own_experts + held * experts) // 128) * 128
     vmem = pl.BlockSpec(memory_space=pltpu.VMEM)
-    served = jax.ShapeDtypeStruct((own_experts, own_hidden, n * width), BF16)
-    return pl.pallas_call(
+    served = pltpu.VMEM((own_experts, own_hidden, n * width), BF16)
+    results = pl.pallas_call(
         functools.partial(
             kernel, rows, n, held * rows, (float(hidden * width * n), float(width * n))
         ),
@@ -243,11 +266,11 @@
             served,
             served,
             served,
-            jax.ShapeDtypeStruct((experts, n * width), BF16),
-            jax.ShapeDtypeStruct((own_experts, 4), F32),
-            jax.ShapeDtypeStruct((held, experts, 4), F32),
+            pltpu.VMEM((experts, n * width), BF16),
+            pltpu.VMEM((own_experts, 4), F32),
+            pltpu.VMEM((held, experts, 4), F32),
         ),
-        in_specs=[pl.BlockSpec(memory_space=pl.ANY)] * 4,
+        in_specs=[pl.BlockSpec(memory_space=pltpu.HBM)] * 4,
         out_specs=(vmem,) * 6,
         scratch_shapes=[
             pltpu.VMEM((3, held, experts, hidden, width), F32),
@@ -267,8 +290,11 @@
             pltpu.SemaphoreType.DMA((5,)),
             pltpu.SemaphoreType.DMA((5,)),
         ],
-        compiler_params=pltpu.CompilerParams(collective_id=0, has_side_effects=True),
+        compiler_params=pltpu.CompilerParams(
+            collective_id=0, has_side_effects=True, vmem_limit_bytes=VMEM_LIMIT
+        ),
     )(rep_w1, rep_w3, rep_w2, rep_gate)
+    return finish(results)
 
 
 def solution(mesh):

time: 18.9 us -> 17.7 us (0.937)
  local copies, waits for them, and re-layouts: 4.59 us -> 3.53 us
    unnamed x16 -> x8, local copies, waits for them, and re-layouts: 4.59 us -> 3.53 us
    pallas_call x0 -> x1, Pallas kernels: none -> 0.7 us  [finish(): pl.pallas_call(finish_kernel, out_shape=tuple((jax.ShapeDtypeStruct(r.sha...]
    pallas_call x1, Pallas kernels: 13.3 us -> 12.6 us  [local(): pl.pallas_call(functools.partial(kernel, rows, n, held * rows, (float(hid...]
where the time goes in v2:
time: 17.7 us; the launch traced here: 17.5 us
  Pallas kernels  13.3 us (75%)
  local copies, waits for them, and re-layouts  3.53 us (20%)
  between operations  0.65 us (4%)
    pallas_call x1, Pallas kernels, local(): pl.pallas_call(functools.partial(kernel, rows, n, held * rows, (float(hid...  12.6 us
    unnamed x8, local copies, waits for them, and re-layouts  3.53 us
    pallas_call x1, Pallas kernels, finish(): pl.pallas_call(finish_kernel, out_shape=tuple((jax.ShapeDtypeStruct(r.sha...  0.7 us

profile of v2, /device:TPU:0, one launch (start us, length us, event | category | flops | bytes accessed | tf_op | source)
XLA Modules:
  0.0 17.5 jit_solution(12707793407517539948)
XLA Ops:
  0.6 0.0 copy-start
  0.6 0.9 %copy-done = f32[2,2,64,256]{3,2,1,0:T(8,128)S(1)} copy-done((f32[2,2,64,256]{3,2,1,0:T(8,128)S(1)}, f32[2,2,64,256]{3,2,1,0:T(8,128)}, u32[]{:S(2)}) %copy-start) | copy-done | bytes 262168
  1.6 0.0 copy-start.1
  1.6 0.9 %copy-done.1 = f32[2,2,64,256]{3,2,1,0:T(8,128)S(1)} copy-done((f32[2,2,64,256]{3,2,1,0:T(8,128)S(1)}, f32[2,2,64,256]{3,2,1,0:T(8,128)}, u32[]{:S(2)}) %copy-start.1) | copy-done | bytes 262168
  2.5 0.0 copy-start.2
  2.5 0.9 %copy-done.2 = f32[2,2,64,256]{3,2,1,0:T(8,128)S(1)} copy-done((f32[2,2,64,256]{3,2,1,0:T(8,128)S(1)}, f32[2,2,64,256]{3,2,1,0:T(8,128)}, u32[]{:S(2)}) %copy-start.2) | copy-done | bytes 262168
  3.5 0.0 copy-start.3
  3.5 0.7 %copy-done.3 = f32[2,2,256]{2,1,0:T(2,128)S(1)} copy-done((f32[2,2,256]{2,1,0:T(2,128)S(1)}, f32[2,2,256]{2,1,0:T(2,128)}, u32[]{:S(2)}) %copy-start.3) | copy-done | bytes 4120
  4.2 12.6 %shard_map.91 = (bf16[1,4,4096]{2,1,0:T(4,128)(2,1)S(1)}, bf16[1,4,4096]{2,1,0:T(4,128)(2,1)S(1)}, bf16[1,4,4096]{2,1,0:T(4,128)(2,1)S(1)}, bf16[2,4096]{1,0:T(2...) custom-call(f32[2,2,64,256]{3,2,1,0:T(8,128)S(1)} %copy-done, f32[2,2,64,256]{3,2,1,0:T(8,128)S(1)} %copy-done.1, ...), custom_call_target="tpu_custom_call" | custom-call | tf_op jit(solution)/shard_map/pallas_call | solution.py:261
  16.8 0.7 %shard_map.92 = (bf16[1,4,4096]{2,1,0:T(4,128)(2,1)}, bf16[1,4,4096]{2,1,0:T(4,128)(2,1)}, bf16[1,4,4096]{2,1,0:T(4,128)(2,1)}, bf16[2,4096]{1,0:T(2,128)(2,1)}, f32[1,4]{1,0:T(1,128)}, /*index=5*/f32[2,2,4]{2,1,0:T(2,128)}) custom-call(bf16[1,4,4096]{2,1,0:T(4,128)(2,1)S(1)} %get-tuple-element.12.refs_0_, ...), custom_call_target="tpu_custom_call" | custom-call | tf_op jit(solution)/shard_map/pallas_call | solution.py:245
Async XLA Ops:
  0.6 1.0 %copy-start = (f32[2,2,64,256]{3,2,1,0:T(8,128)S(1)}, f32[2,2,64,256]{3,2,1,0:T(8,128)}, u32[]{:S(2)}) copy-start(f32[2,2,64,256]{3,2,1,0:T(8,128)} %w1_hbm.1) | copy-start | bytes 786436
  1.6 0.9 %copy-start.1 = (f32[2,2,64,256]{3,2,1,0:T(8,128)S(1)}, f32[2,2,64,256]{3,2,1,0:T(8,128)}, u32[]{:S(2)}) copy-start(f32[2,2,64,256]{3,2,1,0:T(8,128)} %w3_hbm.1) | copy-start | bytes 786436
  2.5 0.9 %copy-start.2 = (f32[2,2,64,256]{3,2,1,0:T(8,128)S(1)}, f32[2,2,64,256]{3,2,1,0:T(8,128)}, u32[]{:S(2)}) copy-start(f32[2,2,64,256]{3,2,1,0:T(8,128)} %w2_hbm.1) | copy-start | bytes 786436
  3.5 0.7 %copy-start.3 = (f32[2,2,256]{2,1,0:T(2,128)S(1)}, f32[2,2,256]{2,1,0:T(2,128)}, u32[]{:S(2)}) copy-start(f32[2,2,256]{2,1,0:T(2,128)} %gate_hbm.1) | copy-start | bytes 12292

commit v3 on v2

--- a/solution.py
+++ b/solution.py
@@ -10,7 +10,7 @@
 MESH = pl.DeviceIdType.MESH
 F32 = jnp.float32
 BF16 = jnp.bfloat16
-VMEM_LIMIT = 40 * 1024 * 1024
+VMEM_LIMIT = 16 * 1024 * 1024
 
 
 def scaled(total, replicas):
@@ -291,7 +291,7 @@
             pltpu.SemaphoreType.DMA((5,)),
         ],
         compiler_params=pltpu.CompilerParams(
-            collective_id=0, has_side_effects=True, vmem_limit_bytes=VMEM_LIMIT
+            collective_id=0, has_side_effects=True
         ),
     )(rep_w1, rep_w3, rep_w2, rep_gate)
     return finish(results)

time: 17.7 us -> 14.2 us (0.80)
  local copies, waits for them, and re-layouts: 3.53 us -> 0 us
    unnamed x8 -> x0, local copies, waits for them, and re-layouts: 3.53 us -> none
where the time goes in v3:
time: 14.2 us; the launch traced here: 14 us
  Pallas kernels  13.4 us (94%)
  between operations  0.64 us (5%)
    pallas_call x1, Pallas kernels, local(): pl.pallas_call(functools.partial(kernel, rows, n, held * rows, (float(hid...  12.7 us
    pallas_call x1, Pallas kernels, finish(): pl.pallas_call(finish_kernel, out_shape=tuple((jax.ShapeDtypeStruct(r.sha...  0.7 us

profile of v3, /device:TPU:0, one launch (start us, length us, event | category | flops | bytes accessed | tf_op | source)
XLA Modules:
  0.0 14.0 jit_solution(331196008132853535)
XLA Ops:
  0.6 12.7 %shard_map.91 = (bf16[1,4,4096]{2,1,0:T(4,128)(2,1)S(1)}, bf16[1,4,4096]{2,1,0:T(4,128)(2,1)S(1)}, bf16[1,4,4096]{2,1,0:T(4,128)(2,1)S(1)}, bf16[2,4096]{1,0:T(2...) custom-call(f32[2,2,64,256]{3,2,1,0:T(8,128)} %w1_hbm.1, f32[2,2,64,256]{3,2,1,0:T(8,128)} %w3_hbm.1, ...), custom_call_target="tpu_custom_call" | custom-call | tf_op jit(solution)/shard_map/pallas_call | solution.py:261
  13.3 0.7 %shard_map.92 = (bf16[1,4,4096]{2,1,0:T(4,128)(2,1)}, bf16[1,4,4096]{2,1,0:T(4,128)(2,1)}, bf16[1,4,4096]{2,1,0:T(4,128)(2,1)}, bf16[2,4096]{1,0:T(2,128)(2,1)}, f32[1,4]{1,0:T(1,128)}, /*index=5*/f32[2,2,4]{2,1,0:T(2,128)}) custom-call(bf16[1,4,4096]{2,1,0:T(4,128)(2,1)S(1)} %get-tuple-element.12.refs_0_, ...), custom_call_target="tpu_custom_call" | custom-call | tf_op jit(solution)/shard_map/pallas_call | solution.py:245
